TPU v7x, 32 devices: a whole 2x2x4 slice. The times are simulated.
32 devices in a mesh: dp: 8 (over z, x), tp: 4 (over y, core).
Axes of the slice: x: 2, y: 2, z: 4, core: 2. Of those that a mesh axis runs over, the one named last changes fastest.
Arguments:
- hidden_in: bfloat16 [512, 3584], P(('dp', 'tp')), may hold values from -6 to 6
- query_latent: bfloat16 [512, 64, 512], P(('dp', 'tp')), may hold values from -348 to 347
- query_rope: bfloat16 [512, 4096], P(('dp', 'tp')), may hold values from -348 to 347
- cache_latent: bfloat16 [512, 128, 512], P(('dp', 'tp')), may hold values from -6 to 6
- cache_rope: bfloat16 [512, 64, 128], P(('dp', 'tp')), may hold values from -6 to 6
- lengths: int32 [512], P(('dp', 'tp')), may hold values from 16 to 128
- value_up: bfloat16 [512, 4096], P(None, 'tp'), may hold values from -1 to 1
- out_proj: bfloat16 [4096, 3584], P('tp'), may hold values from -0.09375 to 0.09375
- norm_gain: float32 [3584], replicated, may hold values from 0.1 to 1.9
- expert_gate: bfloat16 [32, 3584, 1024], P(('dp', 'tp')), may hold values from -0.09375 to 0.09375
- expert_down: bfloat16 [32, 1024, 3584], P(('dp', 'tp')), may hold values from -0.1875 to 0.1875
- expert_ids: int32 [512, 8], P(('dp', 'tp')), may hold values from 0 to 31, all different within a row; in each aligned block of 16 rows (0 to 15, 16 to 31, ...) at most 4 rows name the same one
- affinity: float32 [512, 8], P(('dp', 'tp')), may hold values from 0.05 to 1
Outputs:
- layer_out: bfloat16 [512, 3584], P(('dp', 'tp'))
Inputs may be any that keep to these rules, and one draw needn't show every extreme that they name: `expert_ids`: in each aligned block of 16 rows (the rows of one device) no expert is named by more than 4 rows.
All inputs are finite; a program needn't handle non-finite values.
Results may differ from a plain program's by a relative error of at most 0.0081.
Values may be sent and summed in bfloat16 or wider, within the bound.
A program may use at most 128 MiB of HBM per device.

v0:
```python
import functools

import jax
import jax.numpy as jnp
from jax import lax
from jax.experimental import pallas as pl
from jax.experimental.pallas import tpu as pltpu
from jax.sharding import PartitionSpec as P

score_scale = 192.0 ** (-0.5)
norm_eps = 1e-06
route_scale = 2.5


def attention_kernel(
    batch, tile, query_hbm, rot_ref, cache_hbm, rope_hbm, lengths_ref, hidden_in_hbm, gain_ref,
    up_hbm, proj_hbm, hidden_ref, normed_ref, leaving, arrived, heads, partial, parts, total, up, proj,
    query_ref, cache_ref, rope_ref, hidden_in_ref, weight_sem, input_sem, out_send, out_recv, part_send, part_recv,
):
    toks, head_count, latent = query_hbm.shape
    context = cache_ref.shape[1]
    group = leaving.shape[0]
    local = head_count // group
    width = proj.shape[1]
    me = lax.axis_index("tp")
    input_copies = []
    for number in range(toks // batch):
        span = pl.ds(number * batch, batch)
        pairs = ((query_hbm, query_ref), (cache_hbm, cache_ref), (rope_hbm, rope_ref))
        input_copies.append([
            pltpu.make_async_copy(src.at[span], dst.at[span], input_sem.at[number, index])
            for index, (src, dst) in enumerate(pairs)
        ])
        for copy in input_copies[-1]:
            copy.start()
    hidden_copy = pltpu.make_async_copy(hidden_in_hbm, hidden_in_ref, weight_sem.at[2])
    up_copy = pltpu.make_async_copy(up_hbm, up, weight_sem.at[0])
    proj_copy = pltpu.make_async_copy(proj_hbm, proj, weight_sem.at[1])
    up_copy.start()
    proj_copy.start()
    hidden_copy.start()
    peers = [lax.rem(me + step, group) for step in range(group)]
    barrier = pltpu.get_barrier_semaphore()
    for step in range(1, group):
        pl.semaphore_signal(
            barrier, inc=1, device_id={"tp": peers[step]}, device_id_type=pl.DeviceIdType.MESH
        )

    def remote(src, dst, send, recv, step):
        return pltpu.make_async_remote_copy(
            src_ref=src, dst_ref=dst, send_sem=send, recv_sem=recv,
            device_id={"tp": peers[step]}, device_id_type=pl.DeviceIdType.MESH,
        )

    position = lax.broadcasted_iota(jnp.int32, (head_count, context), 1)
    out_copies = {}
    for first in range(0, toks, batch):
        for copy in input_copies[first // batch]:
            copy.wait()
        scores = []
        for t in range(first, first + batch):
            score = lax.dot_general(
                query_ref[t], cache_ref[t], (((1,), (1,)), ((), ())), preferred_element_type=jnp.float32
            )
            score = score + jnp.dot(rot_ref[t], rope_ref[t], preferred_element_type=jnp.float32)
            scores.append(jnp.where(position < lengths_ref[t], score * score_scale, -jnp.inf))
        weights = []
        for score in scores:
            raised = jnp.exp(score - jnp.max(score, axis=1, keepdims=True))
            weights.append((raised / jnp.sum(raised, axis=1, keepdims=True)).astype(jnp.bfloat16))
        for offset, weight in enumerate(weights):
            t = first + offset
            mixed = jnp.dot(weight, cache_ref[t], preferred_element_type=jnp.float32).astype(jnp.bfloat16)
            for part in range(group):
                leaving[part, t] = mixed[part * local:(part + 1) * local]
        if first == 0:
            pl.semaphore_wait(barrier, group - 1)
        span = pl.ds(first, batch)
        for step in range(1, group):
            number = first // batch
            out_copies[number, step] = remote(
                leaving.at[peers[step], span], arrived.at[step, span],
                out_send.at[number, step], out_recv.at[number, step], step,
            )
            out_copies[number, step].start()

    up_copy.wait()
    head_width = up.shape[1] // local
    lane = lax.broadcasted_iota(jnp.int32, (local, up.shape[1]), 1)
    row = lax.broadcasted_iota(jnp.int32, (local, up.shape[1]), 0)
    own_head = lax.div(lane, head_width) == row
    for step in range(group):
        for first in range(0, toks, batch):
            if step:
                out_copies[first // batch, step].wait_recv()
        source = leaving[me] if step == 0 else arrived[step]
        flat = source.reshape(toks * local, latent)
        for column in range(0, up.shape[1], 256):
            wide = jnp.dot(flat, up[:, column:column + 256], preferred_element_type=jnp.float32)
            wide = wide.reshape(toks, local, 256)
            kept = jnp.where(own_head[None, :, column:column + 256], wide, 0.0)
            heads[step * toks:(step + 1) * toks, column:column + 256] = jnp.sum(kept, axis=1).astype(jnp.bfloat16)
    proj_copy.wait()
    part_copies = {}
    for number in range(width // tile):
        columns = slice(number * tile, (number + 1) * tile)
        product = jnp.dot(heads[...], proj[:, columns], preferred_element_type=jnp.float32)
        total[:, columns] = product[:toks]
        for step in range(1, group):
            partial[number, step] = product[step * toks:(step + 1) * toks].astype(jnp.bfloat16)
            back = group - step
            part_copies[number, step] = remote(
                partial.at[number, step], parts.at[number, step],
                part_send.at[number, step], part_recv.at[number, step], back,
            )
            part_copies[number, step].start()
    hidden_copy.wait()
    squares = jnp.zeros((toks, 1), jnp.float32)
    for number in range(width // tile):
        columns = slice(number * tile, (number + 1) * tile)
        value = total[:, columns]
        for step in range(1, group):
            part_copies[number, step].wait_recv()
            value = value + parts[number, step].astype(jnp.float32)
        low = (hidden_in_ref[:, columns].astype(jnp.float32) + value).astype(jnp.bfloat16)
        hidden_ref[:, columns] = low
        squares = squares + jnp.sum(low.astype(jnp.float32) * low.astype(jnp.float32), axis=1, keepdims=True)
    inv_norm = lax.rsqrt(squares / width + norm_eps)
    normed_ref[...] = (hidden_ref[...].astype(jnp.float32) * inv_norm * gain_ref[...]).astype(jnp.bfloat16)
    for copy in list(out_copies.values()) + list(part_copies.values()):
        copy.wait_send()


def run_attention(query, rot, cache, rope, lengths, hidden_in, gain, value_up, out_proj):
    toks, head_count, latent = query.shape
    group = lax.axis_size("tp")
    local = head_count // group
    width = out_proj.shape[1]
    batch = 4 if toks % 4 == 0 else 1
    tile = 512 if width % 512 == 0 else 128
    tiles = width // tile
    dma = pltpu.SemaphoreType.DMA
    vmem = pl.BlockSpec(memory_space=pltpu.VMEM)
    hbm = pl.BlockSpec(memory_space=pl.ANY)
    smem = pl.BlockSpec(memory_space=pltpu.SMEM)
    low = jnp.bfloat16
    return pl.pallas_call(
        functools.partial(attention_kernel, batch, tile),
        out_shape=[jax.ShapeDtypeStruct((toks, width), low)] * 2,
        in_specs=[hbm, vmem, hbm, hbm, smem, hbm, vmem, hbm, hbm],
        out_specs=[vmem, vmem],
        scratch_shapes=[
            pltpu.VMEM((group, toks, local, latent), low),
            pltpu.VMEM((group, toks, local, latent), low),
            pltpu.VMEM((group * toks, out_proj.shape[0]), low),
            pltpu.VMEM((tiles, group, toks, tile), low),
            pltpu.VMEM((tiles, group, toks, tile), low),
            pltpu.VMEM((toks, width), jnp.float32),
            pltpu.VMEM(value_up.shape, low),
            pltpu.VMEM(out_proj.shape, low),
            pltpu.VMEM(query.shape, low),
            pltpu.VMEM(cache.shape, low),
            pltpu.VMEM(rope.shape, low),
            pltpu.VMEM(hidden_in.shape, low),
            dma((3,)), dma((toks // batch, 3)), dma((toks // batch, group)), dma((toks // batch, group)),
            dma((tiles, group)), dma((tiles, group)),
        ],
        compiler_params=pltpu.CompilerParams(
            collective_id=0, has_side_effects=True, vmem_limit_bytes=60 * 1024 * 1024
        ),
    )(query, rot, cache, rope, lengths, hidden_in, gain, value_up, out_proj)


def per_device(
    hidden_in,
    query_latent,
    query_rope,
    cache_latent,
    cache_rope,
    lengths,
    value_up,
    out_proj,
    norm_gain,
    expert_gate,
    expert_down,
    expert_ids,
    affinity,
):
    toks, head_count, _ = query_latent.shape
    hidden, normed = run_attention(
        query_latent, query_rope.reshape(toks, head_count, -1), cache_latent, cache_rope, lengths,
        hidden_in, norm_gain.reshape(1, -1), value_up, out_proj,
    )
    dp, tp = lax.axis_size("dp"), lax.axis_size("tp")
    inner_dp = 2 if dp % 2 == 0 else 1
    experts = expert_gate.shape[0] * dp * tp
    capacity = max(2, -(-expert_ids.size // experts))
    shape = (dp // inner_dp, inner_dp * tp, inner_dp, tp, capacity)
    route = routing(expert_ids, affinity, shape)
    return run_experts(normed, hidden, expert_gate, expert_down, route, shape)


def experts_kernel(
    shape, normed_ref, hidden_ref, route_ref, gate_hbm, down_hbm, out_ref,
    block, route, sending, received, rows, inner, answers, back, partial, parts,
    gate, down, weight_sem, far_send, far_recv, route_send, route_recv,
    near_send, near_recv, own_sem, back_send, back_recv, part_send, part_recv,
):
    outer, plane, inner_dp, tp, cap = shape
    toks, width = normed_ref.shape
    slots = plane * cap
    at = lax.axis_index("dp")
    level = lax.div(at, inner_dp)
    me = lax.rem(at, inner_dp) * tp + lax.axis_index("tp")
    chunk = 256
    gate_copy = pltpu.make_async_copy(gate_hbm.at[0], gate, weight_sem.at[0])
    down_copy = pltpu.make_async_copy(down_hbm.at[0], down, weight_sem.at[1])
    gate_copy.start()
    down_copy.start()

    def far(step):
        return {"dp": lax.rem(level + step, outer) * inner_dp + lax.rem(at, inner_dp), "tp": lax.axis_index("tp")}

    def near(index):
        return {"dp": level * inner_dp + lax.div(index, tp), "tp": lax.rem(index, tp)}

    def remote(src, dst, send, recv, device):
        return pltpu.make_async_remote_copy(
            src_ref=src, dst_ref=dst, send_sem=send, recv_sem=recv,
            device_id=device, device_id_type=pl.DeviceIdType.MESH,
        )

    barrier = pltpu.get_barrier_semaphore()
    for step in range(1, outer):
        pl.semaphore_signal(barrier, inc=1, device_id=far(step), device_id_type=pl.DeviceIdType.MESH)
    for step in range(1, plane):
        pl.semaphore_signal(
            barrier, inc=1, device_id=near(lax.rem(me + step, plane)), device_id_type=pl.DeviceIdType.MESH
        )
    pl.semaphore_wait(barrier, outer + plane - 2)

    started = []
    far_copies, route_copies = {}, {}
    for step in range(1, outer):
        target = lax.rem(level + step, outer)
        route_copies[step] = remote(
            route_ref.at[target], route.at[step], route_send.at[step], route_recv.at[step], far(step)
        )
        far_copies[step] = remote(normed_ref, block.at[step], far_send.at[step], far_recv.at[step], far(step))
        route_copies[step].start()
        far_copies[step].start()

    near_copies, own_copies = {}, {}
    for step in range(outer):
        if step:
            route_copies[step].wait_recv()
            far_copies[step].wait_recv()
            pick, tokens = route[step, :slots, :toks], block[step]
        else:
            pick, tokens = route_ref[level, :slots, :toks], normed_ref[...]
        picked = jnp.dot(pick, tokens, preferred_element_type=jnp.float32).astype(jnp.bfloat16)
        for index in range(plane):
            sending[step, index] = picked[index * cap:(index + 1) * cap]
        own_copies[step] = pltpu.make_async_copy(sending.at[step, me], received.at[me, step], own_sem.at[step])
        own_copies[step].start()
        for hop in range(1, plane):
            peer = lax.rem(me + hop, plane)
            near_copies[step, hop] = remote(
                sending.at[step, peer], received.at[me, step],
                near_send.at[step, hop], near_recv.at[step, hop], near(peer),
            )
            near_copies[step, hop].start()
    for step in range(outer):
        own_copies[step].wait()
        for hop in range(1, plane):
            near_copies[step, hop].wait_recv()

    for index in range(plane):
        for step in range(outer):
            first = (index * outer + step) * cap
            rows[first:first + cap, :] = received[index, step]
    gate_copy.wait()

    @pl.loop(0, inner.shape[1] // chunk)
    def _(j):
        columns = pl.ds(pl.multiple_of(j * chunk, chunk), chunk)
        pre = jnp.dot(rows[...], gate[:, columns], preferred_element_type=jnp.float32)
        inner[:, columns] = jax.nn.silu(pre).astype(jnp.bfloat16)

    down_copy.wait()

    @pl.loop(0, width // chunk)
    def _(j):
        columns = pl.ds(pl.multiple_of(j * chunk, chunk), chunk)
        answer = jnp.dot(inner[...], down[:, columns], preferred_element_type=jnp.float32).astype(jnp.bfloat16)
        for index in range(plane):
            for step in range(outer):
                first = (index * outer + step) * cap
                answers[step, index, :, columns] = answer[first:first + cap]

    back_copies, own_back = {}, {}
    order = list(range(1, outer)) + [0]
    for step in order:
        for hop in range(1, plane):
            peer = lax.rem(me + hop, plane)
            back_copies[step, hop] = remote(
                answers.at[step, peer], back.at[step, me],
                back_send.at[step, hop], back_recv.at[step, hop], near(peer),
            )
            back_copies[step, hop].start()
        own_back[step] = pltpu.make_async_copy(answers.at[step, me], back.at[step, me], own_sem.at[step])
        own_back[step].start()
    part_copies = {}
    total = hidden_ref[...].astype(jnp.float32)
    for step in order:
        own_back[step].wait()
        for hop in range(1, plane):
            back_copies[step, hop].wait_recv()
        arrived = jnp.concatenate([back[step, index] for index in range(plane)], axis=0)
        if step:
            high, low = route[step, slots:slots + toks, :slots], route[step, slots + toks:, :slots]
        else:
            high, low = route_ref[level, slots:slots + toks, :slots], route_ref[level, slots + toks:, :slots]
        mixed = jnp.dot(high, arrived, preferred_element_type=jnp.float32) + jnp.dot(
            low, arrived, preferred_element_type=jnp.float32
        )
        if step:
            partial[step] = mixed.astype(jnp.bfloat16)
            part_copies[step] = remote(
                partial.at[step], parts.at[step], part_send.at[step], part_recv.at[step], far(outer - step)
            )
            part_copies[step].start()
        else:
            total = total + mixed
    for step in range(1, outer):
        part_copies[step].wait_recv()
        total = total + parts[step].astype(jnp.float32)
    out_ref[...] = total
    for step in range(1, outer):
        route_copies[step].wait_send()
        far_copies[step].wait_send()
        part_copies[step].wait_send()
    for step in range(outer):
        for hop in range(1, plane):
            near_copies[step, hop].wait_send()
            back_copies[step, hop].wait_send()


def run_experts(normed, hidden, expert_gate, expert_down, route, shape):
    outer, plane, _, _, cap = shape
    toks, width = normed.shape
    ff = expert_gate.shape[2]
    count = outer * plane * cap
    dma = pltpu.SemaphoreType.DMA
    vmem = pl.BlockSpec(memory_space=pltpu.VMEM)
    hbm = pl.BlockSpec(memory_space=pl.ANY)
    low = jnp.bfloat16
    return pl.pallas_call(
        functools.partial(experts_kernel, shape),
        out_shape=jax.ShapeDtypeStruct((toks, width), jnp.float32),
        in_specs=[vmem, vmem, vmem, hbm, hbm],
        out_specs=vmem,
        scratch_shapes=[
            pltpu.VMEM((outer, toks, width), low),
            pltpu.VMEM(route.shape, low),
            pltpu.VMEM((outer, plane, cap, width), low),
            pltpu.VMEM((plane, outer, cap, width), low),
            pltpu.VMEM((count, width), low),
            pltpu.VMEM((count, ff), low),
            pltpu.VMEM((outer, plane, cap, width), low),
            pltpu.VMEM((outer, plane, cap, width), low),
            pltpu.VMEM((outer, toks, width), low),
            pltpu.VMEM((outer, toks, width), low),
            pltpu.VMEM(expert_gate.shape[1:], low),
            pltpu.VMEM(expert_down.shape[1:], low),
            dma((2,)), dma((outer,)), dma((outer,)), dma((outer,)), dma((outer,)),
            dma((outer, plane)), dma((outer, plane)), dma((outer,)),
            dma((outer, plane)), dma((outer, plane)), dma((outer,)), dma((outer,)),
        ],
        compiler_params=pltpu.CompilerParams(
            collective_id=2, has_side_effects=True, vmem_limit_bytes=60 * 1024 * 1024
        ),
    )(normed, hidden, route, expert_gate, expert_down).astype(low)


def routing(expert_ids, affinity, shape):
    outer, plane, _, _, cap = shape
    toks = expert_ids.shape[0]
    experts = outer * plane
    weight = route_scale * affinity / jnp.sum(affinity, axis=1, keepdims=True)
    named = expert_ids[:, :, None] == lax.broadcasted_iota(jnp.int32, (1, 1, experts), 2)
    chosen = jnp.sum(named.astype(jnp.int32), axis=1)
    weights = jnp.sum(jnp.where(named, weight[:, :, None], 0.0), axis=1)
    before = lax.broadcasted_iota(jnp.int32, (toks, toks, 1), 1) < lax.broadcasted_iota(
        jnp.int32, (toks, toks, 1), 0
    )
    rank = jnp.sum(jnp.where(before, chosen[None], 0), axis=1)
    rank = jnp.where(chosen > 0, rank, -1)
    in_slot = rank[:, :, None] == lax.broadcasted_iota(jnp.int32, (1, 1, cap), 2)
    in_slot = in_slot.reshape(toks, outer, plane * cap)
    spread = jnp.repeat(weights, cap, axis=1).reshape(toks, outer, plane * cap)
    spread = jnp.where(in_slot, spread, 0.0)
    high = spread.astype(jnp.bfloat16)
    rest = (spread - high.astype(jnp.float32)).astype(jnp.bfloat16)
    lanes = 128 * (-(-max(toks, plane * cap) // 128))

    def padded(array):
        return jnp.pad(array, ((0, 0), (0, 0), (0, lanes - array.shape[2])))

    pick = padded(in_slot.astype(jnp.bfloat16).transpose(1, 2, 0))
    return jnp.concatenate(
        [pick, padded(high.transpose(1, 0, 2)), padded(rest.transpose(1, 0, 2))], axis=1
    )


def solution(mesh):
    return jax.shard_map(
        per_device,
        mesh=mesh,
        in_specs=(
            P(("dp", "tp"), None),
            P(("dp", "tp"), None, None),
            P(("dp", "tp"), None),
            P(("dp", "tp"), None, None),
            P(("dp", "tp"), None, None),
            P(("dp", "tp")),
            P(None, "tp"),
            P("tp", None),
            P(),
            P(("dp", "tp"), None, None),
            P(("dp", "tp"), None, None),
            P(("dp", "tp"), None),
            P(("dp", "tp"), None),
        ),
        out_specs=P(("dp", "tp"), None),
        check_vma=False,
    )
```

profile of v0, /device:TPU:0, one launch (start us, length us, event | category | flops | bytes accessed | tf_op | source)
XLA Modules:
  0.0 79.3 jit_solution(15406731281226934017)
XLA Ops:
  0.0 0.0 copy-start
  0.0 0.0 copy-start.1
  0.0 1.9 %reshape.28.rot_ref = bf16[16,64,64]{2,1,0:T(8,128)(2,1)} reshape(bf16[16,4096]{1,0:T(8,128)(2,1)} %param.15) | data formatting | bytes 262144 | tf_op jit(solution)/shard_map/reshape | solution.py:191
  1.9 1.3 %reshape.29.gain_ref = f32[1,3584]{1,0:T(1,128)} reshape(f32[3584]{0:T(1024)} %param.21) | data formatting | bytes 28672 | tf_op jit(solution)/shard_map/reshape | solution.py:192
  3.2 26.4 %shard_map.127 = (bf16[16,3584]{1,0:T(8,128)(2,1)}, bf16[16,3584]{1,0:T(8,128)(2,1)}) custom-call(bf16[16,64,512]{2,1,0:T(8,128)(2,1)} %query_hbm.1, bf16[16,64,64]{2,1,0:T(8,128)(2,1)} %reshape.28.rot_ref, bf16[16,128,512]{2,1,0:T(8,128)(2,1)} %cache_hbm.1, bf16[16,64,128]{2,1,0:T(8,128)(2,1)} %rope_hbm.1, s32[16]{0:T(128)} %lengths_ref.1, ...), custom_call_target="tpu_custom_call" | custom-call | tf_op jit(solution)/shard_map/pallas_call | solution.py:147
  29.6 0.0 copy-done
  29.6 0.1 copy.33
  29.7 0.0 copy-done.1
  29.7 0.1 copy.30
  29.8 0.1 select_reduce_fusion.1
  29.9 0.1 copy.34
  30.0 0.1 copy.35
  30.1 0.1 convert_reduce_fusion
  30.2 0.1 select_reduce_fusion
  30.3 0.1 copy.31
  30.4 0.1 copy.32
  30.5 0.1 eq.39
  30.7 0.1 copy.36
  30.8 0.6 fusion.4.route_ref
  31.4 46.3 %shard_map.128 = f32[16,3584]{1,0:T(8,128)} custom-call(bf16[16,3584]{1,0:T(8,128)(2,1)} %get-tuple-element.7.normed_ref, bf16[16,3584]{1,0:T(8,128)(2,1)} %get-tuple-element.8.hidden_ref, bf16[4,64,128]{2,1,0:T(8,128)(2,1)} %fusion.4.route_ref, bf16[1,3584,1024]{2,1,0:T(8,128)(2,1)} %gate_hbm.1, bf16[1,1024,3584]{2,1,0:T(8,128)(2,1)} %down_hbm.1), custom_call_target="tpu_custom_call" | custom-call | tf_op jit(solution)/shard_map/pallas_call | solution.py:358
  77.7 1.6 %convert_element_type.25 = bf16[16,3584]{1,0:T(8,128)(2,1)} convert(f32[16,3584]{1,0:T(8,128)} %shard_map.128) | non-fusion elementwise | flops 57344 | bytes 344064 | tf_op jit(solution)/shard_map/convert_element_type | solution.py:383
  (10 shorter events, 0.1 us)
Async XLA Ops:
  0.0 29.6 %copy-start = (f32[16,8]{0,1:T(8,128)S(1)}, f32[16,8]{0,1:T(8,128)}, u32[]{:S(2)}) copy-start(f32[16,8]{0,1:T(8,128)} %param.25) | copy-start | bytes 1540
  0.0 29.7 %copy-start.1 = (s32[16,8]{0,1:T(8,128)S(1)}, s32[16,8]{0,1:T(8,128)}, u32[]{:S(2)}) copy-start(s32[16,8]{0,1:T(8,128)} %param.24) | copy-start | bytes 1540
where the time goes:
time: 79.9 us; the launch traced here: 79.3 us
  Pallas kernels  72.7 us (91%)
  local copies, waits for them, and re-layouts  3.89 us (5%)
  other arithmetic  2.65 us (3%)
    pallas_call x1, Pallas kernels, run_experts(): pl.pallas_call(functools.partial(experts_kernel, shape), out_shape=jax.Sh...  46.3 us
    pallas_call x1, Pallas kernels, run_attention(): pl.pallas_call(functools.partial(attention_kernel, batch, tile), out_shap...  26.4 us
    reshape x1, local copies, waits for them, and re-layouts, per_device(): query_rope.reshape(toks, head_count, -1)  1.91 us

commit v1 on v0

v1 whole, which is shorter than its diff:
```python
import functools
import types

import jax
import jax.numpy as jnp
from jax import lax
from jax.experimental import pallas as pl
from jax.experimental.pallas import tpu as pltpu
from jax.sharding import PartitionSpec as P

score_scale = 192.0 ** (-0.5)
norm_eps = 1e-06
route_scale = 2.5
low = jnp.bfloat16
wide = jnp.float32


def scratch_plan(size):
    tiles, tile, toks, outer, plane, per = size.tiles, size.tile, size.toks, size.outer, size.plane, size.per
    group, local, count = size.group, size.local, size.count
    dma = pltpu.SemaphoreType.DMA
    vmem = pltpu.VMEM
    lanes = size.lanes
    return dict(
        leaving=vmem((group, toks, local, size.latent), low),
        arrived=vmem((group, toks, local, size.latent), low),
        heads=vmem((group * toks, size.depth), low),
        partial=vmem((tiles, group, toks, tile), low),
        parts=vmem((tiles, group, toks, tile), low),
        total=vmem((tiles, toks, tile), wide),
        up=vmem((size.latent, size.depth), low),
        proj=vmem((size.depth, size.width), low),
        query=vmem((toks, size.heads, size.latent), low),
        cache=vmem((toks, size.context, size.latent), low),
        rope=vmem((toks, size.rope, size.context), low),
        rot=vmem((toks, size.heads * size.rope), low),
        turned=vmem((toks, size.heads, 128), low),
        hidden_in=vmem((toks, size.width), low),
        gain=vmem((size.width,), wide),
        meta=vmem((2 * size.topk, lanes), wide),
        meta_in=vmem((outer, 2 * size.topk, lanes), wide),
        pick=vmem((count, lanes), low),
        mix=vmem((2 * outer * toks, count), low),
        block=vmem((tiles, outer * toks, tile), low),
        sending=vmem((tiles, plane, per, tile), low),
        received=vmem((tiles, plane, per, tile), low),
        squares=vmem((count, 128), wide),
        acc=vmem((count, size.ff), wide),
        inner=vmem((count, size.ff), low),
        answers=vmem((tiles, plane, per, tile), low),
        back=vmem((tiles, plane, per, tile), low),
        owed=vmem((tiles, outer, toks, tile), low),
        owing=vmem((tiles, outer, toks, tile), low),
        gate=vmem((size.width, size.ff), low),
        down=vmem((size.ff, size.width), low),
        input_sem=dma((toks // size.batch, 3)),
        load_sem=dma((8,)),
        out_send=dma((toks // size.batch, group)),
        out_recv=dma((toks // size.batch, group)),
        part_send=dma((tiles, group)),
        part_recv=dma((tiles, group)),
        meta_send=dma((outer,)),
        meta_recv=dma((outer,)),
        far_send=dma((tiles, outer)),
        far_recv=dma((tiles, outer)),
        near_send=dma((tiles, plane)),
        near_recv=dma((tiles, plane)),
        back_send=dma((tiles, plane)),
        back_recv=dma((tiles, plane)),
        owed_send=dma((tiles, outer)),
        owed_recv=dma((tiles, outer)),
    )


def layer_kernel(
    size, names, query_hbm, rot_hbm, cache_hbm, rope_hbm, lengths_ref, hidden_hbm, gain_hbm, up_hbm, proj_hbm,
    meta_hbm, gate_hbm, down_hbm, out_ref, *refs,
):
    v = types.SimpleNamespace(**dict(zip(names, refs)))
    toks, batch, group, local, latent = size.toks, size.batch, size.group, size.local, size.latent
    tiles, tile, outer, plane, per, cap, count = (
        size.tiles, size.tile, size.outer, size.plane, size.per, size.cap, size.count
    )
    tp, inner_dp = size.tp, size.inner_dp
    head_count, context = size.heads, size.context
    at, my_tp = lax.axis_index("dp"), lax.axis_index("tp")
    level = lax.div(at, inner_dp)
    me = lax.rem(at, inner_dp) * tp + my_tp

    loads = {}

    def load(index, src, dst):
        loads[index] = pltpu.make_async_copy(src, dst, v.load_sem.at[index])
        loads[index].start()

    load(0, rot_hbm, v.rot)
    input_copies = []
    for number in range(toks // batch):
        span = pl.ds(number * batch, batch)
        pairs = ((query_hbm, v.query), (cache_hbm, v.cache), (rope_hbm, v.rope))
        input_copies.append([
            pltpu.make_async_copy(src.at[span], dst.at[span], v.input_sem.at[number, index])
            for index, (src, dst) in enumerate(pairs)
        ])
        for copy in input_copies[-1]:
            copy.start()
    load(1, meta_hbm, v.meta)
    load(2, up_hbm, v.up)
    load(3, proj_hbm, v.proj)
    load(4, hidden_hbm, v.hidden_in)
    load(5, gain_hbm, v.gain)

    def far(step):
        return {"dp": lax.rem(level + step, outer) * inner_dp + lax.rem(at, inner_dp), "tp": my_tp}

    def near(index):
        return {"dp": level * inner_dp + lax.div(index, tp), "tp": lax.rem(index, tp)}

    tp_peer = [lax.rem(my_tp + step, group) for step in range(group)]
    near_peer = [lax.rem(me + hop, plane) for hop in range(plane)]
    sent = []

    def remote(src, dst, send, recv, device):
        copy = pltpu.make_async_remote_copy(
            src_ref=src, dst_ref=dst, send_sem=send, recv_sem=recv,
            device_id=device, device_id_type=pl.DeviceIdType.MESH,
        )
        copy.start()
        sent.append(copy)
        return copy

    barrier = pltpu.get_barrier_semaphore()
    for step in range(1, outer):
        pl.semaphore_signal(barrier, inc=1, device_id=far(step), device_id_type=pl.DeviceIdType.MESH)
    for hop in range(1, plane):
        pl.semaphore_signal(barrier, inc=1, device_id=near(near_peer[hop]), device_id_type=pl.DeviceIdType.MESH)

    ratio = 128 // size.rope
    strips = head_count // ratio
    loads[0].wait()
    flat_rot = jnp.concatenate([v.rot[:, j * 128:(j + 1) * 128] for j in range(strips)], axis=0)
    spin_rows = batch * head_count
    spin_row = lax.broadcasted_iota(jnp.int32, (spin_rows, 1), 0)
    spin_lane = lax.broadcasted_iota(jnp.int32, (spin_rows, strips * toks), 1)
    head_of = lax.rem(spin_row, head_count)
    lane_of = lax.broadcasted_iota(jnp.int32, (spin_rows, 128), 1)
    own_lanes = lax.div(lane_of, size.rope) == lax.rem(head_of, ratio)
    for first in range(0, toks, batch):
        source = lax.div(head_of, ratio) * toks + lax.div(spin_row, head_count) + first
        spread = jnp.where(spin_lane == source, 1.0, 0.0).astype(low)
        moved = jnp.dot(spread, flat_rot, preferred_element_type=wide)
        moved = jnp.where(own_lanes, moved, 0.0).astype(low)
        v.turned[first:first + batch] = moved.reshape(batch, head_count, 128)

    position = lax.broadcasted_iota(jnp.int32, (head_count, context), 1)
    out_copies, meta_copies = {}, {}
    for first in range(0, toks, batch):
        for copy in input_copies[first // batch]:
            copy.wait()
        scores = []
        for t in range(first, first + batch):
            score = lax.dot_general(
                v.query[t], v.cache[t], (((1,), (1,)), ((), ())), preferred_element_type=wide
            )
            keys = jnp.concatenate([v.rope[t]] * ratio, axis=0)
            score = score + jnp.dot(v.turned[t], keys, preferred_element_type=wide)
            scores.append(jnp.where(position < lengths_ref[t], score * score_scale, -jnp.inf))
        weights = []
        for score in scores:
            raised = jnp.exp(score - jnp.max(score, axis=1, keepdims=True))
            weights.append((raised / jnp.sum(raised, axis=1, keepdims=True)).astype(low))
        for offset, weight in enumerate(weights):
            t = first + offset
            mixed = jnp.dot(weight, v.cache[t], preferred_element_type=wide).astype(low)
            for part in range(group):
                v.leaving[part, t] = mixed[part * local:(part + 1) * local]
        if first == 0:
            pl.semaphore_wait(barrier, outer + plane - 2)
        span = pl.ds(first, batch)
        number = first // batch
        for step in range(1, group):
            out_copies[number, step] = remote(
                v.leaving.at[tp_peer[step], span], v.arrived.at[step, span],
                v.out_send.at[number, step], v.out_recv.at[number, step], {"tp": tp_peer[step]},
            )
        if first == 0:
            loads[1].wait()
            for step in range(1, outer):
                meta_copies[step] = remote(
                    v.meta, v.meta_in.at[step], v.meta_send.at[step], v.meta_recv.at[step], far(step)
                )
            load(6, gate_hbm.at[0], v.gate)
            load(7, down_hbm.at[0], v.down)

    for step in range(1, outer):
        meta_copies[step].wait_recv()
    lanes, topk = size.lanes, size.topk
    step_of = lax.div(lax.broadcasted_iota(jnp.int32, (2 * topk, lanes), 1), toks)
    table = v.meta[...]
    for step in range(1, outer):
        table = jnp.where(step_of == step, v.meta_in[step], table)
    ids, affinity = table[:topk], table[topk:]
    shares = route_scale * affinity / jnp.sum(affinity, axis=0, keepdims=True)
    row = lax.broadcasted_iota(jnp.int32, (count, lanes), 0)
    lane = lax.broadcasted_iota(jnp.int32, (count, lanes), 1)
    expert = (level * plane + lax.div(row, per)).astype(wide)
    chosen = jnp.zeros((count, lanes), wide)
    share = jnp.zeros((count, lanes), wide)
    for k in range(topk):
        hit = ids[k:k + 1] == expert
        chosen = jnp.where(hit, 1.0, chosen)
        share = jnp.where(hit, shares[k:k + 1], share)
    older = lax.broadcasted_iota(jnp.int32, (lanes, lanes), 0)
    newer = lax.broadcasted_iota(jnp.int32, (lanes, lanes), 1)
    before = (older < newer) & (lax.div(older, toks) == lax.div(newer, toks))
    rank = jnp.dot(chosen.astype(low), jnp.where(before, 1.0, 0.0).astype(low), preferred_element_type=wide)
    slot = lax.rem(row, cap).astype(wide)
    own_step = lax.div(lane, toks) == lax.rem(lax.div(row, cap), outer)
    held = (chosen > 0.5) & own_step & (rank == slot)
    v.pick[...] = jnp.where(held, 1.0, 0.0).astype(low)
    flipped = jnp.where(held, share, 0.0).T
    high = flipped.astype(low)
    v.mix[:outer * toks] = high[:outer * toks]
    v.mix[outer * toks:] = (flipped - high.astype(wide)).astype(low)[:outer * toks]

    loads[2].wait()
    head_width = size.depth // local
    lane = lax.broadcasted_iota(jnp.int32, (local, size.depth), 1)
    row = lax.broadcasted_iota(jnp.int32, (local, size.depth), 0)
    own_head = lax.div(lane, head_width) == row
    for step in range(group):
        for first in range(0, toks, batch):
            if step:
                out_copies[first // batch, step].wait_recv()
        source = v.leaving[my_tp] if step == 0 else v.arrived[step]
        flat = source.reshape(toks * local, latent)
        for column in range(0, size.depth, 256):
            product = jnp.dot(flat, v.up[:, column:column + 256], preferred_element_type=wide)
            product = product.reshape(toks, local, 256)
            kept = jnp.where(own_head[None, :, column:column + 256], product, 0.0)
            v.heads[step * toks:(step + 1) * toks, column:column + 256] = jnp.sum(kept, axis=1).astype(low)
    loads[3].wait()
    part_copies = {}
    for n in range(tiles):
        product = jnp.dot(v.heads[...], v.proj[:, n * tile:(n + 1) * tile], preferred_element_type=wide)
        v.total[n] = product[:toks]
        for step in range(1, group):
            v.partial[n, step] = product[step * toks:(step + 1) * toks].astype(low)
            part_copies[n, step] = remote(
                v.partial.at[n, step], v.parts.at[n, step],
                v.part_send.at[n, step], v.part_recv.at[n, step], {"tp": tp_peer[group - step]},
            )
    loads[4].wait()
    far_copies = {}
    for n in range(tiles):
        value = v.total[n]
        for step in range(1, group):
            part_copies[n, step].wait_recv()
            value = value + v.parts[n, step].astype(wide)
        hidden = (v.hidden_in[:, n * tile:(n + 1) * tile].astype(wide) + value).astype(low)
        v.block[n, :toks] = hidden
        for step in range(1, outer):
            far_copies[n, step] = remote(
                v.block.at[n, pl.ds(0, toks)], v.block.at[n, pl.ds(step * toks, toks)],
                v.far_send.at[n, step], v.far_recv.at[n, step], far(step),
            )

    near_copies = {}

    def dispatch(n):
        for step in range(1, outer):
            far_copies[n, step].wait_recv()
        picked = jnp.dot(v.pick[:, :outer * toks], v.block[n], preferred_element_type=wide).astype(low)
        v.sending[n] = picked.reshape(plane, per, tile)
        for hop in range(1, plane):
            near_copies[n, hop] = remote(
                v.sending.at[n, near_peer[hop]], v.received.at[n, me],
                v.near_send.at[n, hop], v.near_recv.at[n, hop], near(near_peer[hop]),
            )
        v.received[n, me] = v.sending[n, me]

    def consume(n):
        for hop in range(1, plane):
            near_copies[n, hop].wait_recv()
        rows = v.received[n].reshape(count, tile).astype(wide)
        square = rows * rows
        folded = square[:, :128]
        for first in range(128, tile, 128):
            folded = folded + square[:, first:first + 128]
        gain = v.gain[pl.ds(n * tile, tile)]
        scaled = (rows * gain[None, :]).astype(low)
        product = jnp.dot(scaled, v.gate[n * tile:(n + 1) * tile, :], preferred_element_type=wide)
        if n == 0:
            v.squares[...] = folded
            v.acc[...] = product
        else:
            v.squares[...] += folded
            v.acc[...] += product

    loads[5].wait()
    lag = 3
    for n in range(tiles + lag):
        if n < tiles:
            dispatch(n)
        if n == lag:
            loads[6].wait()
        if n >= lag:
            consume(n - lag)
    inv_norm = lax.rsqrt(jnp.sum(v.squares[...], axis=1, keepdims=True) / size.width + norm_eps)
    v.inner[...] = jax.nn.silu(v.acc[...] * inv_norm).astype(low)
    loads[7].wait()

    back_copies, owed_copies = {}, {}
    for n in range(tiles):
        answer = jnp.dot(v.inner[...], v.down[:, n * tile:(n + 1) * tile], preferred_element_type=wide).astype(low)
        v.answers[n] = answer.reshape(plane, per, tile)
        for hop in range(1, plane):
            back_copies[n, hop] = remote(
                v.answers.at[n, near_peer[hop]], v.back.at[n, me],
                v.back_send.at[n, hop], v.back_recv.at[n, hop], near(near_peer[hop]),
            )
        v.back[n, me] = v.answers[n, me]

    def combine(n):
        for hop in range(1, plane):
            back_copies[n, hop].wait_recv()
        mixed = jnp.dot(v.mix[...], v.back[n].reshape(count, tile), preferred_element_type=wide)
        mixed = mixed[:outer * toks] + mixed[outer * toks:]
        v.total[n] = v.block[n, :toks].astype(wide) + mixed[:toks]
        for step in range(1, outer):
            v.owed[n, step] = mixed[step * toks:(step + 1) * toks].astype(low)
            owed_copies[n, step] = remote(
                v.owed.at[n, step], v.owing.at[n, step],
                v.owed_send.at[n, step], v.owed_recv.at[n, step], far(outer - step),
            )

    def finish(n):
        value = v.total[n]
        for step in range(1, outer):
            owed_copies[n, step].wait_recv()
            value = value + v.owing[n, step].astype(wide)
        out_ref[:, n * tile:(n + 1) * tile] = value.astype(low)

    for n in range(tiles + lag):
        if n < tiles:
            combine(n)
        if n >= lag:
            finish(n - lag)
    for copy in sent:
        copy.wait_send()


def per_device(
    hidden_in,
    query_latent,
    query_rope,
    cache_latent,
    cache_rope,
    lengths,
    value_up,
    out_proj,
    norm_gain,
    expert_gate,
    expert_down,
    expert_ids,
    affinity,
):
    toks, head_count, latent = query_latent.shape
    dp, tp = lax.axis_size("dp"), lax.axis_size("tp")
    inner_dp = 2 if dp % 2 == 0 else 1
    outer, plane = dp // inner_dp, inner_dp * tp
    experts = expert_gate.shape[0] * dp * tp
    cap = max(2, -(-expert_ids.size // experts))
    width, ff = expert_gate.shape[1:]
    tile = 512 if width % 512 == 0 else 128
    topk = expert_ids.shape[1]
    lanes = 128 * (-(-outer * toks // 128))
    size = types.SimpleNamespace(
        toks=toks, heads=head_count, latent=latent, context=cache_latent.shape[1], rope=cache_rope.shape[1],
        depth=out_proj.shape[0], width=width, ff=ff, group=tp, local=head_count // tp, tp=tp, inner_dp=inner_dp,
        outer=outer, plane=plane, cap=cap, per=outer * cap, count=plane * outer * cap, tile=tile,
        tiles=width // tile, batch=4 if toks % 4 == 0 else 1, topk=topk, lanes=lanes,
    )
    meta = jnp.concatenate([expert_ids.T.astype(wide), affinity.T], axis=0)
    meta = jnp.tile(meta, (1, lanes // toks))
    plan = scratch_plan(size)
    hbm = pl.BlockSpec(memory_space=pl.ANY)
    return pl.pallas_call(
        functools.partial(layer_kernel, size, tuple(plan)),
        out_shape=jax.ShapeDtypeStruct((toks, width), low),
        in_specs=[hbm] * 4 + [pl.BlockSpec(memory_space=pltpu.SMEM)] + [hbm] * 7,
        out_specs=pl.BlockSpec(memory_space=pltpu.VMEM),
        scratch_shapes=list(plan.values()),
        compiler_params=pltpu.CompilerParams(
            collective_id=0, has_side_effects=True, vmem_limit_bytes=60 * 1024 * 1024
        ),
    )(
        query_latent, query_rope, cache_latent, cache_rope, lengths, hidden_in, norm_gain, value_up, out_proj,
        meta, expert_gate, expert_down,
    )


def solution(mesh):
    spread = P(("dp", "tp"))
    return jax.shard_map(
        per_device,
        mesh=mesh,
        in_specs=(
            spread, spread, spread, spread, spread, spread, P(None, "tp"), P("tp", None), P(), spread, spread,
            spread, spread,
        ),
        out_specs=spread,
        check_vma=False,
    )
```

time: 79.9 us -> 66 us (0.83)
  Pallas kernels: 72.7 us -> 62.1 us
  local copies, waits for them, and re-layouts: 3.89 us -> 2.24 us
  other arithmetic: 2.65 us -> 1.38 us
    pallas_call x2 -> x1, Pallas kernels: 72.7 us -> 62.1 us  [per_device(): pl.pallas_call(functools.partial(layer_kernel, size, tuple(plan)), out_sh...]
    reshape x2 -> x0, local copies, waits for them, and re-layouts: 3.24 us -> none  [the longest x1 1.91 us: per_device(): query_rope.reshape(toks, head_count, -1)]
    unnamed x5 -> x1, local copies, waits for them, and re-layouts: 0.08 us -> 1.55 us
    convert_element_type x1, other arithmetic: 1.6 us -> 0.69 us  [per_device(): meta = jnp.concatenate([expert_ids.T.astype(wide), affinity.T], axis=0)]
where the time goes in v1:
time: 66 us; the launch traced here: 65.7 us
  Pallas kernels  62.1 us (94%)
  local copies, waits for them, and re-layouts  2.24 us (3%)
  other arithmetic  1.38 us (2%)
    pallas_call x1, Pallas kernels, per_device(): pl.pallas_call(functools.partial(layer_kernel, size, tuple(plan)), out_sh...  62.1 us
    unnamed x1, local copies, waits for them, and re-layouts  1.55 us

profile of v1, /device:TPU:0, one launch (start us, length us, event | category | flops | bytes accessed | tf_op | source)
XLA Modules:
  0.0 65.7 jit_solution(13146408742705298631)
XLA Ops:
  0.0 0.7 %convert_bitcast_fusion = f32[8,16]{1,0:T(8,128)S(1)} fusion(s32[16,8]{0,1:T(8,128)} %param.24), kind=kLoop, calls=%fused_computation.1 | loop fusion | flops 128 | bytes 1024 | tf_op jit(solution)/shard_map/convert_element_type | solution.py:384
  0.7 0.7 %pad_maximum_fusion = f32[16,16]{1,0:T(8,128)S(1)} fusion(f32[8,16]{1,0:T(8,128)} %bitcast.3, f32[8,16]{1,0:T(8,128)S(1)} %convert_bitcast_fusion), kind=kLoop, calls=%fused_computation | loop fusion | flops 256 | bytes 2048 | tf_op jit(solution)/shard_map/concatenate | solution.py:384
  1.4 0.7 %tile.10.meta_hbm = f32[16,128]{1,0:T(8,128)} reshape(f32[16,8,16]{2,1,0:T(8,128)S(1)} %tile.4) | data formatting | bytes 16384 | tf_op jit(solution)/shard_map/tile | solution.py:385
  2.1 62.1 %shard_map.127 = bf16[16,3584]{1,0:T(8,128)(2,1)} custom-call(bf16[16,64,512]{2,1,0:T(8,128)(2,1)} %query_hbm.1, bf16[16,4096]{1,0:T(8,128)(2,1)} %rot_hbm.1, bf16[16,128,512]{2,1,0:T(8,128)(2,1)} %cache_hbm.1, bf16[16,64,128]{2,1,0:T(8,128)(2,1)} %rope_hbm.1, s32[16]{0:T(128)} %lengths_ref.1, bf16[16,3584]{1,0:T(8,128)(2,1)} %hidden_hbm.1, f32[3584]{0:T(1024)} %gain_hbm.1, ...), custom_call_target="tpu_custom_call" | custom-call | tf_op jit(solution)/shard_map/pallas_call | solution.py:388
  64.2 1.6 %copy.15 = bf16[16,3584]{1,0:T(8,128)(2,1)} copy(bf16[16,3584]{1,0:T(8,128)(2,1)} %shard_map.127) | data formatting | bytes 229376
  (1 shorter events, 0.0 us)

commit v2 on v1

v2 whole, which is shorter than its diff:
```python
import functools
import types

import jax
import jax.numpy as jnp
from jax import lax
from jax.experimental import pallas as pl
from jax.experimental.pallas import tpu as pltpu
from jax.sharding import PartitionSpec as P

score_scale = 192.0 ** (-0.5)
norm_eps = 1e-06
route_scale = 2.5
low = jnp.bfloat16
wide = jnp.float32


def scratch_plan(size):
    tiles, tile, toks, outer, plane, per = size.tiles, size.tile, size.toks, size.outer, size.plane, size.per
    group, local, count = size.group, size.local, size.count
    dma = pltpu.SemaphoreType.DMA
    vmem = pltpu.VMEM
    lanes = size.lanes
    return dict(
        leaving=vmem((group, toks, local, size.latent), low),
        arrived=vmem((group, toks, local, size.latent), low),
        heads=vmem((group * toks, size.depth), low),
        partial=vmem((tiles, 2, toks, tile), low),
        parts=vmem((tiles, 2, toks, tile), low),
        across=vmem((tiles, toks, tile), wide),
        crossing=vmem((tiles, toks, tile), low),
        crossed=vmem((tiles, toks, tile), low),
        total=vmem((tiles, toks, tile), wide),
        up=vmem((size.latent, size.depth), low),
        proj=vmem((size.depth, size.width), low),
        query=vmem((toks, size.heads, size.latent), low),
        cache=vmem((toks, size.context, size.latent), low),
        rope=vmem((toks, size.rope, size.context), low),
        rot=vmem((toks, size.heads * size.rope), low),
        hidden_in=vmem((toks, size.width), low),
        gain=vmem((size.width,), wide),
        ids=vmem((size.topk, toks), jnp.int32),
        affinity=vmem((size.topk, toks), wide),
        meta=vmem((2 * size.topk, lanes), wide),
        meta_in=vmem((outer, 2 * size.topk, lanes), wide),
        pick=vmem((count, lanes), low),
        mix=vmem((2 * outer * toks, count), low),
        block=vmem((tiles, outer * toks, tile), low),
        sending=vmem((tiles, plane, per, tile), low),
        received=vmem((tiles, plane, per, tile), low),
        squares=vmem((count, 128), wide),
        acc=vmem((count, size.ff), wide),
        inner=vmem((count, size.ff), low),
        answers=vmem((tiles, plane, per, tile), low),
        back=vmem((tiles, plane, per, tile), low),
        owed=vmem((tiles, outer, toks, tile), low),
        owing=vmem((tiles, outer, toks, tile), low),
        gate=vmem((size.width, size.ff), low),
        down=vmem((size.ff, size.width), low),
        lengths=pltpu.SMEM((toks,), jnp.int32),
        input_sem=dma((len(size.spans), 3)),
        load_sem=dma((10,)),
        send_sem=dma((8,)),
        out_recv=dma((size.halves, group)),
        pair_recv=dma((tiles,)),
        part_recv=dma((tiles,)),
        far_recv=dma((tiles,)),
        near_recv=dma((tiles,)),
        back_recv=dma((tiles,)),
        owed_recv=dma((tiles,)),
    )


def layer_kernel(
    size, names, query_hbm, rot_hbm, cache_hbm, rope_hbm, lengths_hbm, hidden_hbm, gain_hbm, up_hbm, proj_hbm,
    ids_hbm, affinity_hbm, gate_hbm, down_hbm, out_ref, *refs,
):
    v = types.SimpleNamespace(**dict(zip(names, refs)))
    toks, batch, group, local, latent = size.toks, size.batch, size.group, size.local, size.latent
    tiles, tile, outer, plane, per, cap, count = (
        size.tiles, size.tile, size.outer, size.plane, size.per, size.cap, size.count
    )
    tp, inner_dp = size.tp, size.inner_dp
    head_count, context = size.heads, size.context
    at, my_tp = lax.axis_index("dp"), lax.axis_index("tp")
    level = lax.div(at, inner_dp)
    me = lax.rem(at, inner_dp) * tp + my_tp

    def far(step):
        return {"dp": lax.rem(level + step, outer) * inner_dp + lax.rem(at, inner_dp), "tp": my_tp}

    def near(index):
        return {"dp": level * inner_dp + lax.div(index, tp), "tp": lax.rem(index, tp)}

    tp_peer = [my_tp, my_tp + 1 - 2 * lax.rem(my_tp, 2), lax.rem(my_tp + 2, 4), 3 - my_tp]
    near_peer = [lax.rem(me + hop, plane) for hop in range(plane)]

    def remote(src, dst, kind, recv, device):
        pltpu.make_async_remote_copy(
            src_ref=src, dst_ref=dst, send_sem=v.send_sem.at[kind], recv_sem=recv,
            device_id=device, device_id_type=pl.DeviceIdType.MESH,
        ).start()

    def settle(like, sem):
        pltpu.make_async_copy(like, like, sem).wait()

    barrier = pltpu.get_barrier_semaphore()
    for step in range(1, outer):
        pl.semaphore_signal(barrier, inc=1, device_id=far(step), device_id_type=pl.DeviceIdType.MESH)
    for hop in range(1, plane):
        pl.semaphore_signal(barrier, inc=1, device_id=near(near_peer[hop]), device_id_type=pl.DeviceIdType.MESH)

    loads = {}

    def load(index, src, dst):
        loads[index] = pltpu.make_async_copy(src, dst, v.load_sem.at[index])
        loads[index].start()

    load(0, rot_hbm, v.rot)
    load(9, lengths_hbm, v.lengths)
    input_copies = []
    for number, (first, extent) in enumerate(size.spans):
        span = pl.ds(first, extent)
        pairs = ((query_hbm, v.query), (cache_hbm, v.cache), (rope_hbm, v.rope))
        input_copies.append([
            pltpu.make_async_copy(src.at[span], dst.at[span], v.input_sem.at[number, index])
            for index, (src, dst) in enumerate(pairs)
        ])
        for copy in input_copies[-1]:
            copy.start()
    load(1, ids_hbm, v.ids)
    load(8, affinity_hbm, v.affinity)

    ratio = 128 // size.rope
    strips = head_count // ratio
    loads[0].wait()
    flat_rot = jnp.concatenate([v.rot[:, j * 128:(j + 1) * 128] for j in range(strips)], axis=0)
    spin_rows = batch * head_count
    spin_row = lax.broadcasted_iota(jnp.int32, (spin_rows, 1), 0)
    spin_lane = lax.broadcasted_iota(jnp.int32, (spin_rows, strips * toks), 1)
    head_of = lax.rem(spin_row, head_count)
    lane_of = lax.broadcasted_iota(jnp.int32, (spin_rows, 128), 1)
    own_lanes = lax.div(lane_of, size.rope) == lax.rem(head_of, ratio)

    def turned(first):
        source = lax.div(head_of, ratio) * toks + lax.div(spin_row, head_count) + first
        spread = jnp.where(spin_lane == source, 1.0, 0.0).astype(low)
        moved = jnp.dot(spread, flat_rot, preferred_element_type=wide)
        return jnp.where(own_lanes, moved, 0.0).astype(low).reshape(batch, head_count, 128)

    half = toks // size.halves
    position = lax.broadcasted_iota(jnp.int32, (head_count, context), 1)
    for first in range(0, toks, batch):
        spun = turned(first)
        for number, (begin, _) in enumerate(size.spans):
            if begin == first:
                for copy in input_copies[number]:
                    copy.wait()
        if first == 0:
            loads[9].wait()
            load(2, up_hbm, v.up)
            load(3, proj_hbm, v.proj)
            load(4, hidden_hbm, v.hidden_in)
            load(5, gain_hbm, v.gain)
        scores = []
        for t in range(first, first + batch):
            score = lax.dot_general(
                v.query[t], v.cache[t], (((1,), (1,)), ((), ())), preferred_element_type=wide
            )
            keys = jnp.concatenate([v.rope[t]] * ratio, axis=0)
            score = score + jnp.dot(spun[t - first], keys, preferred_element_type=wide)
            scores.append(jnp.where(position < v.lengths[t], score * score_scale, -jnp.inf))
        weights = []
        for score in scores:
            raised = jnp.exp(score - jnp.max(score, axis=1, keepdims=True))
            weights.append((raised / jnp.sum(raised, axis=1, keepdims=True)).astype(low))
        for offset, weight in enumerate(weights):
            t = first + offset
            mixed = jnp.dot(weight, v.cache[t], preferred_element_type=wide).astype(low)
            for part in range(group):
                v.leaving[part, t] = mixed[part * local:(part + 1) * local]
        if first == 0:
            pl.semaphore_wait(barrier, outer + plane - 2)
        span = pl.ds(first, batch)
        for step in range(group - 1, 0, -1):
            remote(
                v.leaving.at[tp_peer[step], span], v.arrived.at[step, span], 0,
                v.out_recv.at[first // half, step], {"tp": tp_peer[step]},
            )
        if first == 0:
            loads[1].wait()
            loads[8].wait()
            spot = lax.broadcasted_iota(jnp.int32, (toks, size.lanes), 0)
            copied = lax.rem(lax.broadcasted_iota(jnp.int32, (toks, size.lanes), 1), toks) == spot
            copied = jnp.where(copied, 1.0, 0.0)
            v.meta[:size.topk] = jnp.dot(
                v.ids[...].astype(wide), copied, precision=lax.Precision.HIGHEST, preferred_element_type=wide
            )
            v.meta[size.topk:] = jnp.dot(
                v.affinity[...], copied, precision=lax.Precision.HIGHEST, preferred_element_type=wide
            )
            for step in range(1, outer):
                remote(v.meta, v.meta_in.at[step], 1, v.out_recv.at[0, 0], far(step))
            load(6, gate_hbm.at[0], v.gate)
            load(7, down_hbm.at[0], v.down)

    settle(v.meta_in.at[pl.ds(1, outer - 1)], v.out_recv.at[0, 0])
    lanes, topk = size.lanes, size.topk
    step_of = lax.div(lax.broadcasted_iota(jnp.int32, (2 * topk, lanes), 1), toks)
    table = v.meta[...]
    for step in range(1, outer):
        table = jnp.where(step_of == step, v.meta_in[step], table)
    ids, affinity = table[:topk], table[topk:]
    shares = route_scale * affinity / jnp.sum(affinity, axis=0, keepdims=True)
    row = lax.broadcasted_iota(jnp.int32, (count, lanes), 0)
    lane = lax.broadcasted_iota(jnp.int32, (count, lanes), 1)
    expert = (level * plane + lax.div(row, per)).astype(wide)
    chosen = jnp.zeros((count, lanes), wide)
    share = jnp.zeros((count, lanes), wide)
    for k in range(topk):
        hit = ids[k:k + 1] == expert
        chosen = jnp.where(hit, 1.0, chosen)
        share = jnp.where(hit, shares[k:k + 1], share)
    older = lax.broadcasted_iota(jnp.int32, (lanes, lanes), 0)
    newer = lax.broadcasted_iota(jnp.int32, (lanes, lanes), 1)
    before = (older < newer) & (lax.div(older, toks) == lax.div(newer, toks))
    rank = jnp.dot(chosen.astype(low), jnp.where(before, 1.0, 0.0).astype(low), preferred_element_type=wide)
    slot = lax.rem(row, cap).astype(wide)
    own_step = lax.div(lane, toks) == lax.rem(lax.div(row, cap), outer)
    held = (chosen > 0.5) & own_step & (rank == slot)
    v.pick[...] = jnp.where(held, 1.0, 0.0).astype(low)
    flipped = jnp.where(held, share, 0.0).T
    high = flipped.astype(low)
    v.mix[:outer * toks] = high[:outer * toks]
    v.mix[outer * toks:] = (flipped - high.astype(wide)).astype(low)[:outer * toks]

    loads[2].wait()
    head_width = size.depth // local
    lane = lax.broadcasted_iota(jnp.int32, (local, size.depth), 1)
    row = lax.broadcasted_iota(jnp.int32, (local, size.depth), 0)
    own_head = lax.div(lane, head_width) == row
    for step in range(group):
        for begin in range(0, toks, half):
            span = pl.ds(begin, half)
            if step:
                settle(v.arrived.at[step, span], v.out_recv.at[begin // half, step])
            source = v.leaving[my_tp, span] if step == 0 else v.arrived[step, span]
            flat = source.reshape(half * local, latent)
            for column in range(0, size.depth, 256):
                product = jnp.dot(flat, v.up[:, column:column + 256], preferred_element_type=wide)
                product = product.reshape(half, local, 256)
                kept = jnp.where(own_head[None, :, column:column + 256], product, 0.0)
                value = jnp.sum(kept, axis=1).astype(low)
                v.heads[step * toks + begin:step * toks + begin + half, column:column + 256] = value
    loads[3].wait()

    def project(n):
        product = jnp.dot(v.heads[...], v.proj[:, n * tile:(n + 1) * tile], preferred_element_type=wide)
        v.total[n] = product[:toks]
        v.across[n] = product[2 * toks:3 * toks]
        v.partial[n, 0] = product[toks:2 * toks].astype(low)
        v.partial[n, 1] = product[3 * toks:].astype(low)
        remote(v.partial.at[n], v.parts.at[n], 2, v.pair_recv.at[n], {"tp": tp_peer[1]})

    def pass_on(n):
        settle(v.parts.at[n], v.pair_recv.at[n])
        v.total[n] += v.parts[n, 0].astype(wide)
        v.crossing[n] = (v.across[n] + v.parts[n, 1].astype(wide)).astype(low)
        remote(v.crossing.at[n], v.crossed.at[n], 3, v.part_recv.at[n], {"tp": tp_peer[2]})

    ahead = 3
    for n in range(tiles + ahead):
        if n < tiles:
            project(n)
        if n >= ahead:
            pass_on(n - ahead)
    loads[4].wait()
    for n in range(tiles):
        settle(v.crossed.at[n], v.part_recv.at[n])
        value = v.total[n] + v.crossed[n].astype(wide)
        hidden = (v.hidden_in[:, n * tile:(n + 1) * tile].astype(wide) + value).astype(low)
        v.block[n, :toks] = hidden
        for step in range(1, outer):
            remote(
                v.block.at[n, pl.ds(0, toks)], v.block.at[n, pl.ds(step * toks, toks)], 4, v.far_recv.at[n], far(step)
            )

    def dispatch(n):
        settle(v.block.at[n, pl.ds(toks, (outer - 1) * toks)], v.far_recv.at[n])
        picked = jnp.dot(v.pick[:, :outer * toks], v.block[n], preferred_element_type=wide).astype(low)
        v.sending[n] = picked.reshape(plane, per, tile)
        for hop in range(1, plane):
            remote(
                v.sending.at[n, near_peer[hop]], v.received.at[n, me], 5, v.near_recv.at[n], near(near_peer[hop])
            )
        v.received[n, me] = v.sending[n, me]

    def consume(n):
        settle(v.received.at[n, pl.ds(1, plane - 1)], v.near_recv.at[n])
        rows = v.received[n].reshape(count, tile).astype(wide)
        square = rows * rows
        folded = square[:, :128]
        for first in range(128, tile, 128):
            folded = folded + square[:, first:first + 128]
        gain = v.gain[pl.ds(n * tile, tile)]
        scaled = (rows * gain[None, :]).astype(low)
        product = jnp.dot(scaled, v.gate[n * tile:(n + 1) * tile, :], preferred_element_type=wide)
        if n == 0:
            v.squares[...] = folded
            v.acc[...] = product
        else:
            v.squares[...] += folded
            v.acc[...] += product

    loads[5].wait()
    lag = 3
    for n in range(tiles + lag):
        if n < tiles:
            dispatch(n)
        if n == lag:
            loads[6].wait()
        if n >= lag:
            consume(n - lag)
    inv_norm = lax.rsqrt(jnp.sum(v.squares[...], axis=1, keepdims=True) / size.width + norm_eps)
    v.inner[...] = jax.nn.silu(v.acc[...] * inv_norm).astype(low)
    loads[7].wait()

    for n in range(tiles):
        answer = jnp.dot(v.inner[...], v.down[:, n * tile:(n + 1) * tile], preferred_element_type=wide).astype(low)
        v.answers[n] = answer.reshape(plane, per, tile)
        for hop in range(1, plane):
            remote(v.answers.at[n, near_peer[hop]], v.back.at[n, me], 6, v.back_recv.at[n], near(near_peer[hop]))
        v.back[n, me] = v.answers[n, me]

    def combine(n):
        settle(v.back.at[n, pl.ds(1, plane - 1)], v.back_recv.at[n])
        mixed = jnp.dot(v.mix[...], v.back[n].reshape(count, tile), preferred_element_type=wide)
        mixed = mixed[:outer * toks] + mixed[outer * toks:]
        v.total[n] = v.block[n, :toks].astype(wide) + mixed[:toks]
        for step in range(1, outer):
            v.owed[n, step] = mixed[step * toks:(step + 1) * toks].astype(low)
            remote(v.owed.at[n, step], v.owing.at[n, step], 7, v.owed_recv.at[n], far(outer - step))

    def finish(n):
        value = v.total[n]
        settle(v.owing.at[n, pl.ds(1, outer - 1)], v.owed_recv.at[n])
        for step in range(1, outer):
            value = value + v.owing[n, step].astype(wide)
        out_ref[:, n * tile:(n + 1) * tile] = value.astype(low)

    for n in range(tiles + lag):
        if n < tiles:
            combine(n)
        if n >= lag:
            finish(n - lag)
    others = pl.ds(0, plane - 1)
    for kind, like in enumerate((
        v.leaving.at[pl.ds(0, group - 1)], v.meta_in.at[pl.ds(0, outer - 1)], v.partial, v.crossing,
        v.block.at[:, pl.ds(0, (outer - 1) * toks)], v.sending.at[:, others], v.answers.at[:, others],
        v.owed.at[:, pl.ds(0, outer - 1)],
    )):
        settle(like, v.send_sem.at[kind])


def per_device(
    hidden_in,
    query_latent,
    query_rope,
    cache_latent,
    cache_rope,
    lengths,
    value_up,
    out_proj,
    norm_gain,
    expert_gate,
    expert_down,
    expert_ids,
    affinity,
):
    toks, head_count, latent = query_latent.shape
    dp, tp = lax.axis_size("dp"), lax.axis_size("tp")
    inner_dp = 2 if dp % 2 == 0 else 1
    outer, plane = dp // inner_dp, inner_dp * tp
    experts = expert_gate.shape[0] * dp * tp
    cap = max(2, -(-expert_ids.size // experts))
    width, ff = expert_gate.shape[1:]
    tile = 512 if width % 512 == 0 else 128
    topk = expert_ids.shape[1]
    batch = 2 if toks % 2 == 0 else 1
    spans = [(0, batch), (batch, toks - batch)]
    if toks % 8 == 0:
        spans = [(0, batch), (batch, 4 - batch), (4, 4), (8, toks - 8)]
    lanes = 128 * (-(-outer * toks // 128))
    size = types.SimpleNamespace(
        toks=toks, heads=head_count, latent=latent, context=cache_latent.shape[1], rope=cache_rope.shape[1],
        depth=out_proj.shape[0], width=width, ff=ff, group=tp, local=head_count // tp, tp=tp, inner_dp=inner_dp,
        outer=outer, plane=plane, cap=cap, per=outer * cap, count=plane * outer * cap, tile=tile,
        tiles=width // tile, batch=batch, spans=spans, halves=2 if toks % 4 == 0 else 1, topk=topk, lanes=lanes,
    )
    plan = scratch_plan(size)
    hbm = pl.BlockSpec(memory_space=pl.ANY)
    return pl.pallas_call(
        functools.partial(layer_kernel, size, tuple(plan)),
        out_shape=jax.ShapeDtypeStruct((toks, width), low),
        in_specs=[hbm] * 13,
        out_specs=pl.BlockSpec(memory_space=pltpu.VMEM),
        scratch_shapes=list(plan.values()),
        compiler_params=pltpu.CompilerParams(
            collective_id=0, has_side_effects=True, vmem_limit_bytes=60 * 1024 * 1024
        ),
    )(
        query_latent, query_rope, cache_latent, cache_rope, lengths, hidden_in, norm_gain, value_up, out_proj,
        expert_ids.T, affinity.T, expert_gate, expert_down,
    )


def solution(mesh):
    spread = P(("dp", "tp"))
    return jax.shard_map(
        per_device,
        mesh=mesh,
        in_specs=(
            spread, spread, spread, spread, spread, spread, P(None, "tp"), P("tp", None), P(), spread, spread,
            spread, spread,
        ),
        out_specs=spread,
        check_vma=False,
    )
```

time: 66 us -> 60.5 us (0.917)
  Pallas kernels: 62.1 us -> 58.8 us
  other arithmetic: 1.38 us -> 0 us
  local copies, waits for them, and re-layouts: 2.24 us -> 1.55 us
    pallas_call x1, Pallas kernels: 62.1 us -> 58.8 us  [per_device(): pl.pallas_call(functools.partial(layer_kernel, size, tuple(plan)), out_sh...]
    concatenate x1 -> x0, other arithmetic: 0.69 us -> none  [per_device(): meta = jnp.concatenate([expert_ids.T.astype(wide), affinity.T], axis=0)]
    another operation x2 -> x0, local copies, waits for them, and re-layouts: 0.69 us -> none  [per_device(): meta = jnp.tile(meta, (1, lanes // toks))]
    convert_element_type x1 -> x0, other arithmetic: 0.69 us -> none  [per_device(): meta = jnp.concatenate([expert_ids.T.astype(wide), affinity.T], axis=0)]
where the time goes in v2:
time: 60.5 us; the launch traced here: 60.4 us
  Pallas kernels  58.8 us (97%)
  local copies, waits for them, and re-layouts  1.55 us (3%)
    pallas_call x1, Pallas kernels, per_device(): pl.pallas_call(functools.partial(layer_kernel, size, tuple(plan)), out_sh...  58.8 us
    unnamed x1, local copies, waits for them, and re-layouts  1.55 us

profile of v2, /device:TPU:0, one launch (start us, length us, event | category | flops | bytes accessed | tf_op | source)
XLA Modules:
  0.0 60.4 jit_solution(14140582133927899083)
XLA Ops:
  0.0 58.8 %shard_map.127 = bf16[16,3584]{1,0:T(8,128)(2,1)} custom-call(bf16[16,64,512]{2,1,0:T(8,128)(2,1)} %query_hbm.1, bf16[16,4096]{1,0:T(8,128)(2,1)} %rot_hbm.1, bf16[16,128,512]{2,1,0:T(8,128)(2,1)} %cache_hbm.1, bf16[16,64,128]{2,1,0:T(8,128)(2,1)} %rope_hbm.1, s32[16]{0:T(128)} %lengths_hbm.1, bf16[16,3584]{1,0:T(8,128)(2,1)} %hidden_hbm.1, f32[3584]{0:T(1024)} %gain_hbm.1, ...), custom_call_target="tpu_custom_call" | custom-call | tf_op jit(solution)/shard_map/pallas_call | solution.py:402
  58.8 1.6 %copy.15 = bf16[16,3584]{1,0:T(8,128)(2,1)} copy(bf16[16,3584]{1,0:T(8,128)(2,1)} %shard_map.127) | data formatting | bytes 229376

commit v3 on v2

--- a/solution.py
+++ b/solution.py
@@ -16,7 +16,7 @@
 
 
 def scratch_plan(size):
-    tiles, tile, toks, outer, plane, per = size.tiles, size.tile, size.toks, size.outer, size.plane, size.per
+    tiles, tile, toks, outer, plane, cap = size.tiles, size.tile, size.toks, size.outer, size.plane, size.cap
     group, local, count = size.group, size.local, size.count
     dma = pltpu.SemaphoreType.DMA
     vmem = pltpu.VMEM
@@ -46,13 +46,18 @@
         pick=vmem((count, lanes), low),
         mix=vmem((2 * outer * toks, count), low),
         block=vmem((tiles, outer * toks, tile), low),
-        sending=vmem((tiles, plane, per, tile), low),
-        received=vmem((tiles, plane, per, tile), low),
+        own_out=vmem((tiles, plane, cap, tile), low),
+        own_in=vmem((tiles, plane, cap, tile), low),
+        far_out=vmem((tiles, plane, outer - 1, cap, tile), low),
+        far_in=vmem((tiles, plane, outer - 1, cap, tile), low),
+        rows=vmem((2, count, tile), low),
         squares=vmem((count, 128), wide),
         acc=vmem((count, size.ff), wide),
         inner=vmem((count, size.ff), low),
-        answers=vmem((tiles, plane, per, tile), low),
-        back=vmem((tiles, plane, per, tile), low),
+        own_answers=vmem((tiles, plane, cap, tile), low),
+        own_back=vmem((tiles, plane, cap, tile), low),
+        far_answers=vmem((tiles, plane, outer - 1, cap, tile), low),
+        far_back=vmem((tiles, plane, outer - 1, cap, tile), low),
         owed=vmem((tiles, outer, toks, tile), low),
         owing=vmem((tiles, outer, toks, tile), low),
         gate=vmem((size.width, size.ff), low),
@@ -60,13 +65,13 @@
         lengths=pltpu.SMEM((toks,), jnp.int32),
         input_sem=dma((len(size.spans), 3)),
         load_sem=dma((10,)),
-        send_sem=dma((8,)),
+        send_sem=dma((10,)),
         out_recv=dma((size.halves, group)),
         pair_recv=dma((tiles,)),
         part_recv=dma((tiles,)),
-        far_recv=dma((tiles,)),
-        near_recv=dma((tiles,)),
-        back_recv=dma((tiles,)),
+        far_recv=dma((tiles, 2)),
+        near_recv=dma((tiles, 2)),
+        back_recv=dma((tiles, 2)),
         owed_recv=dma((tiles,)),
     )
 
@@ -77,9 +82,7 @@
 ):
     v = types.SimpleNamespace(**dict(zip(names, refs)))
     toks, batch, group, local, latent = size.toks, size.batch, size.group, size.local, size.latent
-    tiles, tile, outer, plane, per, cap, count = (
-        size.tiles, size.tile, size.outer, size.plane, size.per, size.cap, size.count
-    )
+    tiles, tile, outer, plane, cap, count = size.tiles, size.tile, size.outer, size.plane, size.cap, size.count
     tp, inner_dp = size.tp, size.inner_dp
     head_count, context = size.heads, size.context
     at, my_tp = lax.axis_index("dp"), lax.axis_index("tp")
@@ -214,7 +217,11 @@
     shares = route_scale * affinity / jnp.sum(affinity, axis=0, keepdims=True)
     row = lax.broadcasted_iota(jnp.int32, (count, lanes), 0)
     lane = lax.broadcasted_iota(jnp.int32, (count, lanes), 1)
-    expert = (level * plane + lax.div(row, per)).astype(wide)
+    mine = plane * cap
+    rest = row - mine
+    near_index = jnp.where(row < mine, lax.div(row, cap), lax.div(rest, (outer - 1) * cap))
+    row_step = jnp.where(row < mine, 0, 1 + lax.rem(lax.div(rest, cap), outer - 1))
+    expert = (level * plane + near_index).astype(wide)
     chosen = jnp.zeros((count, lanes), wide)
     share = jnp.zeros((count, lanes), wide)
     for k in range(topk):
@@ -226,7 +233,7 @@
     before = (older < newer) & (lax.div(older, toks) == lax.div(newer, toks))
     rank = jnp.dot(chosen.astype(low), jnp.where(before, 1.0, 0.0).astype(low), preferred_element_type=wide)
     slot = lax.rem(row, cap).astype(wide)
-    own_step = lax.div(lane, toks) == lax.rem(lax.div(row, cap), outer)
+    own_step = lax.div(lane, toks) == row_step
     held = (chosen > 0.5) & own_step & (rank == slot)
     v.pick[...] = jnp.where(held, 1.0, 0.0).astype(low)
     flipped = jnp.where(held, share, 0.0).T
@@ -274,30 +281,77 @@
             project(n)
         if n >= ahead:
             pass_on(n - ahead)
-    loads[4].wait()
-    for n in range(tiles):
+    line = outer == 4
+    edge = (level == 0) | (level == outer - 1)
+
+    def to_level(n, step):
+        remote(v.block.at[n, pl.ds(0, toks)], v.block.at[n, pl.ds(step * toks, toks)], 4, v.far_recv.at[n, step % 2], far(step))
+
+    def near_sends(out, into, kind, recv):
+        for hop in range(1, plane):
+            remote(out.at[near_peer[hop]], into.at[me], kind, recv, near(near_peer[hop]))
+
+    def residual(n):
         settle(v.crossed.at[n], v.part_recv.at[n])
         value = v.total[n] + v.crossed[n].astype(wide)
         hidden = (v.hidden_in[:, n * tile:(n + 1) * tile].astype(wide) + value).astype(low)
         v.block[n, :toks] = hidden
         for step in range(1, outer):
-            remote(
-                v.block.at[n, pl.ds(0, toks)], v.block.at[n, pl.ds(step * toks, toks)], 4, v.far_recv.at[n], far(step)
-            )
+            if line and step == 1:
+                pl.when(level != outer - 1)(functools.partial(to_level, n, step))
+            elif line and step == outer - 1:
+                pl.when(level != 0)(functools.partial(to_level, n, step))
+            else:
+                to_level(n, step)
+        picked = jnp.dot(v.pick[:mine, :toks], hidden, preferred_element_type=wide).astype(low)
+        for index in range(plane):
+            v.own_out[n, index] = picked[index * cap:(index + 1) * cap]
+        near_sends(v.own_out.at[n], v.own_in.at[n], 5, v.near_recv.at[n, 0])
+        v.own_in[n, me] = v.own_out[n, me]
+
+    def relay(n):
+        settle(v.block.at[n, pl.ds(0, (outer // 2 - (0 if outer % 2 else 1)) * toks)], v.far_recv.at[n, 0])
+        if line:
+            def pass_up():
+                remote(
+                    v.block.at[n, pl.ds(2 * toks, toks)], v.block.at[n, pl.ds(3 * toks, toks)], 4,
+                    v.far_recv.at[n, 1], far(1),
+                )
+
+            def pass_down():
+                remote(
+                    v.block.at[n, pl.ds(2 * toks, toks)], v.block.at[n, pl.ds(toks, toks)], 4,
+                    v.far_recv.at[n, 1], far(3),
+                )
+
+            pl.when(level == 2)(pass_up)
+            pl.when(level == 1)(pass_down)
 
     def dispatch(n):
-        settle(v.block.at[n, pl.ds(toks, (outer - 1) * toks)], v.far_recv.at[n])
-        picked = jnp.dot(v.pick[:, :outer * toks], v.block[n], preferred_element_type=wide).astype(low)
-        v.sending[n] = picked.reshape(plane, per, tile)
-        for hop in range(1, plane):
-            remote(
-                v.sending.at[n, near_peer[hop]], v.received.at[n, me], 5, v.near_recv.at[n], near(near_peer[hop])
-            )
-        v.received[n, me] = v.sending[n, me]
+        settle(v.block.at[n, pl.ds(0, outer // 2 * toks)], v.far_recv.at[n, 1])
+        picked = jnp.dot(
+            v.pick[mine:, :outer * toks], v.block[n], preferred_element_type=wide
+        ).astype(low)
+        for index in range(plane):
+            for step in range(outer - 1):
+                first = (index * (outer - 1) + step) * cap
+                v.far_out[n, index, step] = picked[first:first + cap]
+        near_sends(v.far_out.at[n], v.far_in.at[n], 6, v.near_recv.at[n, 1])
+        v.far_in[n, me] = v.far_out[n, me]
+
+    def gather(own, distant, into):
+        for index in range(plane):
+            into[index * cap:(index + 1) * cap] = own[index]
+            for step in range(outer - 1):
+                first = mine + (index * (outer - 1) + step) * cap
+                into[first:first + cap] = distant[index, step]
 
     def consume(n):
-        settle(v.received.at[n, pl.ds(1, plane - 1)], v.near_recv.at[n])
-        rows = v.received[n].reshape(count, tile).astype(wide)
+        settle(v.own_in.at[n, pl.ds(0, plane - 1)], v.near_recv.at[n, 0])
+        settle(v.far_in.at[n, pl.ds(0, plane - 1)], v.near_recv.at[n, 1])
+        into = v.rows.at[n % 2]
+        gather(v.own_in.at[n], v.far_in.at[n], into)
+        rows = into[...].astype(wide)
         square = rows * rows
         folded = square[:, :128]
         for first in range(128, tile, 128):
@@ -312,13 +366,17 @@
             v.squares[...] += folded
             v.acc[...] += product
 
+    loads[4].wait()
+    for n in range(tiles):
+        residual(n)
     loads[5].wait()
-    lag = 3
+    loads[6].wait()
+    behind, lag = 1, 4
     for n in range(tiles + lag):
         if n < tiles:
-            dispatch(n)
-        if n == lag:
-            loads[6].wait()
+            relay(n)
+        if behind <= n < tiles + behind:
+            dispatch(n - behind)
         if n >= lag:
             consume(n - lag)
     inv_norm = lax.rsqrt(jnp.sum(v.squares[...], axis=1, keepdims=True) / size.width + norm_eps)
@@ -327,39 +385,59 @@
 
     for n in range(tiles):
         answer = jnp.dot(v.inner[...], v.down[:, n * tile:(n + 1) * tile], preferred_element_type=wide).astype(low)
-        v.answers[n] = answer.reshape(plane, per, tile)
-        for hop in range(1, plane):
-            remote(v.answers.at[n, near_peer[hop]], v.back.at[n, me], 6, v.back_recv.at[n], near(near_peer[hop]))
-        v.back[n, me] = v.answers[n, me]
+        for index in range(plane):
+            v.own_answers[n, index] = answer[index * cap:(index + 1) * cap]
+            for step in range(outer - 1):
+                first = mine + (index * (outer - 1) + step) * cap
+                v.far_answers[n, index, step] = answer[first:first + cap]
+        near_sends(v.far_answers.at[n], v.far_back.at[n], 7, v.back_recv.at[n, 1])
+        v.far_back[n, me] = v.far_answers[n, me]
+    for n in range(tiles):
+        near_sends(v.own_answers.at[n], v.own_back.at[n], 8, v.back_recv.at[n, 0])
+        v.own_back[n, me] = v.own_answers[n, me]
 
     def combine(n):
-        settle(v.back.at[n, pl.ds(1, plane - 1)], v.back_recv.at[n])
-        mixed = jnp.dot(v.mix[...], v.back[n].reshape(count, tile), preferred_element_type=wide)
+        settle(v.far_back.at[n, pl.ds(0, plane - 1)], v.back_recv.at[n, 1])
+        into = v.rows.at[n % 2]
+        for index in range(plane):
+            for step in range(outer - 1):
+                first = mine + (index * (outer - 1) + step) * cap
+                into[first:first + cap] = v.far_back[n, index, step]
+        mixed = jnp.dot(v.mix[:, mine:], into[mine:], preferred_element_type=wide)
         mixed = mixed[:outer * toks] + mixed[outer * toks:]
-        v.total[n] = v.block[n, :toks].astype(wide) + mixed[:toks]
         for step in range(1, outer):
             v.owed[n, step] = mixed[step * toks:(step + 1) * toks].astype(low)
-            remote(v.owed.at[n, step], v.owing.at[n, step], 7, v.owed_recv.at[n], far(outer - step))
+            remote(v.owed.at[n, step], v.owing.at[n, step], 9, v.owed_recv.at[n], far(outer - step))
 
     def finish(n):
-        value = v.total[n]
+        settle(v.own_back.at[n, pl.ds(0, plane - 1)], v.back_recv.at[n, 0])
+        into = v.rows.at[n % 2]
+        for index in range(plane):
+            into[index * cap:(index + 1) * cap] = v.own_back[n, index]
+        mixed = jnp.dot(v.mix[:, :mine], into[:mine], preferred_element_type=wide)
+        value = v.block[n, :toks].astype(wide) + mixed[:toks] + mixed[outer * toks:outer * toks + toks]
         settle(v.owing.at[n, pl.ds(1, outer - 1)], v.owed_recv.at[n])
         for step in range(1, outer):
             value = value + v.owing[n, step].astype(wide)
         out_ref[:, n * tile:(n + 1) * tile] = value.astype(low)
 
-    for n in range(tiles + lag):
-        if n < tiles:
-            combine(n)
-        if n >= lag:
-            finish(n - lag)
+    for n in range(tiles):
+        combine(n)
+    for n in range(tiles):
+        finish(n)
     others = pl.ds(0, plane - 1)
     for kind, like in enumerate((
         v.leaving.at[pl.ds(0, group - 1)], v.meta_in.at[pl.ds(0, outer - 1)], v.partial, v.crossing,
-        v.block.at[:, pl.ds(0, (outer - 1) * toks)], v.sending.at[:, others], v.answers.at[:, others],
-        v.owed.at[:, pl.ds(0, outer - 1)],
+        None, v.own_out.at[:, others], v.far_out.at[:, others], v.far_answers.at[:, others],
+        v.own_answers.at[:, others], v.owed.at[:, pl.ds(0, outer - 1)],
     )):
-        settle(like, v.send_sem.at[kind])
+        if like is not None:
+            settle(like, v.send_sem.at[kind])
+    if line:
+        pl.when(edge)(lambda: settle(v.block.at[:, pl.ds(0, 2 * toks)], v.send_sem.at[4]))
+        pl.when(jnp.logical_not(edge))(lambda: settle(v.block, v.send_sem.at[4]))
+    else:
+        settle(v.block.at[:, pl.ds(0, (outer - 1) * toks)], v.send_sem.at[4])
 
 
 def per_device(
@@ -394,14 +472,14 @@
     size = types.SimpleNamespace(
         toks=toks, heads=head_count, latent=latent, context=cache_latent.shape[1], rope=cache_rope.shape[1],
         depth=out_proj.shape[0], width=width, ff=ff, group=tp, local=head_count // tp, tp=tp, inner_dp=inner_dp,
-        outer=outer, plane=plane, cap=cap, per=outer * cap, count=plane * outer * cap, tile=tile,
+        outer=outer, plane=plane, cap=cap, count=plane * outer * cap, tile=tile,
         tiles=width // tile, batch=batch, spans=spans, halves=2 if toks % 4 == 0 else 1, topk=topk, lanes=lanes,
     )
     plan = scratch_plan(size)
     hbm = pl.BlockSpec(memory_space=pl.ANY)
     return pl.pallas_call(
         functools.partial(layer_kernel, size, tuple(plan)),
-        out_shape=jax.ShapeDtypeStruct((toks, width), low),
+        out_shape=pltpu.VMEM((toks, width), low),
         in_specs=[hbm] * 13,
         out_specs=pl.BlockSpec(memory_space=pltpu.VMEM),
         scratch_shapes=list(plan.values()),

time: 60.5 us -> 56.7 us (0.937)
  Pallas kernels: 58.8 us -> 55.9 us
  local copies, waits for them, and re-layouts: 1.55 us -> 0.65 us
    pallas_call x1, Pallas kernels: 58.8 us -> 55.9 us  [per_device(): pl.pallas_call(functools.partial(layer_kernel, size, tuple(plan)), out_sh...]
    unnamed x1, local copies, waits for them, and re-layouts: 1.55 us -> 0.65 us
where the time goes in v3:
time: 56.7 us; the launch traced here: 56.6 us
  Pallas kernels  55.9 us (99%)
  local copies, waits for them, and re-layouts  0.65 us (1%)
    pallas_call x1, Pallas kernels, per_device(): pl.pallas_call(functools.partial(layer_kernel, size, tuple(plan)), out_sh...  55.9 us

profile of v3, /device:TPU:0, one launch (start us, length us, event | category | flops | bytes accessed | tf_op | source)
XLA Modules:
  0.0 56.6 jit_solution(14357331085051026602)
XLA Ops:
  0.0 55.9 %shard_map.127 = bf16[16,3584]{1,0:T(8,128)(2,1)S(1)} custom-call(bf16[16,64,512]{2,1,0:T(8,128)(2,1)} %query_hbm.1, bf16[16,4096]{1,0:T(8,128)(2,1)} %rot_hbm.1, bf16[16,128,512]{2,1,0:T(8,128)(2,1)} %cache_hbm.1, bf16[16,64,128]{2,1,0:T(8,128)(2,1)} %rope_hbm.1, s32[16]{0:T(128)} %lengths_hbm.1, bf16[16,3584]{1,0:T(8,128)(2,1)} %hidden_hbm.1, ...), custom_call_target="tpu_custom_call" | custom-call | tf_op jit(solution)/shard_map/pallas_call | solution.py:480
  55.9 0.6 %copy.15 = bf16[16,3584]{1,0:T(8,128)(2,1)} copy(bf16[16,3584]{1,0:T(8,128)(2,1)S(1)} %shard_map.127) | data formatting | bytes 229376

commit v4 on v3

--- a/solution.py
+++ b/solution.py
@@ -246,19 +246,21 @@
     lane = lax.broadcasted_iota(jnp.int32, (local, size.depth), 1)
     row = lax.broadcasted_iota(jnp.int32, (local, size.depth), 0)
     own_head = lax.div(lane, head_width) == row
-    for step in range(group):
-        for begin in range(0, toks, half):
-            span = pl.ds(begin, half)
-            if step:
-                settle(v.arrived.at[step, span], v.out_recv.at[begin // half, step])
-            source = v.leaving[my_tp, span] if step == 0 else v.arrived[step, span]
-            flat = source.reshape(half * local, latent)
-            for column in range(0, size.depth, 256):
-                product = jnp.dot(flat, v.up[:, column:column + 256], preferred_element_type=wide)
-                product = product.reshape(half, local, 256)
-                kept = jnp.where(own_head[None, :, column:column + 256], product, 0.0)
-                value = jnp.sum(kept, axis=1).astype(low)
-                v.heads[step * toks + begin:step * toks + begin + half, column:column + 256] = value
+    begins = range(0, toks, half)
+    order = [(step, begin) for step in (0, 1) for begin in begins]
+    order += [(step, begin) for begin in begins for step in (2, 3)]
+    for step, begin in order:
+        span = pl.ds(begin, half)
+        if step:
+            settle(v.arrived.at[step, span], v.out_recv.at[begin // half, step])
+        source = v.leaving[my_tp, span] if step == 0 else v.arrived[step, span]
+        flat = source.reshape(half * local, latent)
+        for column in range(0, size.depth, 256):
+            product = jnp.dot(flat, v.up[:, column:column + 256], preferred_element_type=wide)
+            product = product.reshape(half, local, 256)
+            kept = jnp.where(own_head[None, :, column:column + 256], product, 0.0)
+            value = jnp.sum(kept, axis=1).astype(low)
+            v.heads[step * toks + begin:step * toks + begin + half, column:column + 256] = value
     loads[3].wait()
 
     def project(n):
@@ -371,7 +373,7 @@
         residual(n)
     loads[5].wait()
     loads[6].wait()
-    behind, lag = 1, 4
+    behind, lag = 0, 3
     for n in range(tiles + lag):
         if n < tiles:
             relay(n)
@@ -405,7 +407,7 @@
                 into[first:first + cap] = v.far_back[n, index, step]
         mixed = jnp.dot(v.mix[:, mine:], into[mine:], preferred_element_type=wide)
         mixed = mixed[:outer * toks] + mixed[outer * toks:]
-        for step in range(1, outer):
+        for step in sorted(range(1, outer), key=lambda step: step != 2):
             v.owed[n, step] = mixed[step * toks:(step + 1) * toks].astype(low)
             remote(v.owed.at[n, step], v.owing.at[n, step], 9, v.owed_recv.at[n], far(outer - step))
 

time: 56.7 us -> 55.9 us (0.986)
  Pallas kernels: 55.9 us -> 55.1 us
    pallas_call x1, Pallas kernels: 55.9 us -> 55.1 us  [per_device(): pl.pallas_call(functools.partial(layer_kernel, size, tuple(plan)), out_sh...]
where the time goes in v4:
time: 55.9 us; the launch traced here: 55.8 us
  Pallas kernels  55.1 us (99%)
  local copies, waits for them, and re-layouts  0.65 us (1%)
    pallas_call x1, Pallas kernels, per_device(): pl.pallas_call(functools.partial(layer_kernel, size, tuple(plan)), out_sh...  55.1 us

profile of v4, /device:TPU:0, one launch (start us, length us, event | category | flops | bytes accessed | tf_op | source)
XLA Modules:
  0.0 55.8 jit_solution(9184122394603663914)
XLA Ops:
  0.0 55.1 %shard_map.127 = bf16[16,3584]{1,0:T(8,128)(2,1)S(1)} custom-call(bf16[16,64,512]{2,1,0:T(8,128)(2,1)} %query_hbm.1, bf16[16,4096]{1,0:T(8,128)(2,1)} %rot_hbm.1, bf16[16,128,512]{2,1,0:T(8,128)(2,1)} %cache_hbm.1, bf16[16,64,128]{2,1,0:T(8,128)(2,1)} %rope_hbm.1, s32[16]{0:T(128)} %lengths_hbm.1, bf16[16,3584]{1,0:T(8,128)(2,1)} %hidden_hbm.1, ...), custom_call_target="tpu_custom_call" | custom-call | tf_op jit(solution)/shard_map/pallas_call | solution.py:482
  55.1 0.6 %copy.15 = bf16[16,3584]{1,0:T(8,128)(2,1)} copy(bf16[16,3584]{1,0:T(8,128)(2,1)S(1)} %shard_map.127) | data formatting | bytes 229376
